TPU v7x, 512 devices: a 4x2x32 block of a 4x8x32 slice. The times are simulated.
512 devices in a mesh: grp: 2 (over y), row: 32 (over z), col: 4 (over x), sub: 2 (over core).
Axes of the slice: x: 4, y: 2, z: 32, core: 2. Of those that a mesh axis runs over, the one named last changes fastest.
The devices are a block of a 4x8x32 slice.
Arguments:
- pair: bfloat16 [768, 384, 128], P(('grp', 'row'), 'col'), parts along dimension 0, may hold values from -6 to 6
- length: int32 [2], P('grp'), parts along dimension 0, may hold values from 192 to 384
- chain: int32 [768], P('grp'), parts along dimension 0, may hold values from 0 to 3, never falling along the last dimension, each value on 1 to 192 neighbouring positions
- att_proj: bfloat16 [128, 4, 128], P(None, None, 'sub'), may hold values from -0.5 to 0.5
- att_bias: bfloat16 [128, 4], P(None, 'sub')
- chain_bias: float32 [4], P('sub'), may hold values from -2 to 2
- att_out: bfloat16 [128, 128], P('sub'), may hold values from -0.5 to 0.5
- mult_in: bfloat16 [128, 512], replicated, may hold values from -0.5 to 0.5
- mult_gate: bfloat16 [128, 128], replicated, may hold values from -0.5 to 0.5
- mult_out: bfloat16 [128, 128], replicated, may hold values from -0.5 to 0.5
- trans_up: bfloat16 [128, 512], replicated, may hold values from -0.5 to 0.5
- trans_down: bfloat16 [512, 128], replicated, may hold values from -0.25 to 0.25
Outputs:
- pair_out: bfloat16 [768, 384, 128], P(('grp', 'row'), ('col', 'sub')), parts along dimension 0
There are 2 independent parts, one for each index of `grp`. A program takes and returns all parts, laid end to end along the dimension named above; an argument that names none is the same for every part. Nothing has to cross between parts.
Inputs may be any that keep to these rules, and one draw needn't show every extreme that they name: chain numbers never fall along the residues; each chain has 1 to 192 residues.
All inputs are finite; a program needn't handle non-finite values.
Results may differ from a plain program's by a relative error of at most 0.012.
The roundings to bfloat16 on the way count: a program that leaves them out, or rounds other values in their place, can miss the bound.
Values may be sent and summed in bfloat16 or wider, within the bound.
A program may use at most 64 MiB of HBM per device.

v0:
```python
import jax
import jax.numpy as jnp
from jax import lax
from jax.sharding import PartitionSpec as P


def sent_together(arrays, axis, dim, along):
    ends, at = ([], 0)
    for a in arrays[:-1]:
        at += a.shape[along]
        ends.append(at)
    both = jnp.concatenate(arrays, axis=along)
    return tuple(jnp.split(lax.all_gather(both, axis, axis=dim, tiled=True), ends, axis=along))


def joined_along(blocks, dim):
    shape = list(blocks.shape[1:])
    shape[dim] *= blocks.shape[0]
    return jnp.moveaxis(blocks, 0, dim).reshape(shape)


def copy_for_each(shard, axis):
    devices = lax.axis_size(axis)
    return lax.all_to_all(
        jnp.broadcast_to(shard[None], (devices, *shard.shape)), axis, 0, 0, tiled=True
    )


def collect(shard, axis, dim):
    return joined_along(copy_for_each(shard, axis), dim)


def cut_along(shard, dim, devices):
    before, after = (shard.shape[:dim], shard.shape[dim + 1 :])
    return jnp.moveaxis(shard.reshape(*before, devices, -1, *after), dim, 0)


def sum_at_owner(shard, axis, dim):
    devices = lax.axis_size(axis)
    blocks = lax.all_to_all(cut_along(shard, dim, devices), axis, 0, 0, tiled=True)
    return jnp.sum(blocks.astype(jnp.float32), axis=0)


def norm(value):
    mean = jnp.mean(value, axis=-1, keepdims=True)
    centred = value - mean
    variance = jnp.mean(centred * centred, axis=-1, keepdims=True)
    return centred * lax.rsqrt(variance + 1e-05)


def local(
    pair,
    length,
    chain,
    att_proj,
    att_bias,
    chain_bias,
    att_out,
    mult_in,
    mult_gate,
    mult_out,
    trans_up,
    trans_down,
):
    rows, cols, width = pair.shape
    row_count = lax.axis_size("row")
    sub_count = lax.axis_size("sub")
    row_index = lax.axis_index("row")
    col_index = lax.axis_index("col")
    sub_index = lax.axis_index("sub")
    total = rows * row_count
    half = cols // sub_count
    heads_here = att_bias.shape[1]
    spread = att_out.shape[0]
    head_dim = spread // heads_here
    mult_width = mult_out.shape[0]
    valid = (jnp.arange(total) < length[0]).astype(jnp.float32)
    normed = norm(pair.astype(jnp.float32)).astype(jnp.bfloat16)
    flat = normed.reshape(rows * cols, width)
    projected = jnp.dot(
        flat, att_proj.reshape(width, 4 * spread), preferred_element_type=jnp.float32
    ).reshape(rows, cols, 4, spread)
    query = (projected[:, :, 0] * head_dim ** (-0.5)).astype(jnp.bfloat16)
    keys = projected[:, :, 1].astype(jnp.bfloat16)
    values = projected[:, :, 2].astype(jnp.bfloat16)
    gating = jax.nn.sigmoid(projected[:, :, 3])
    bias_local = (
        jnp.dot(flat, att_bias, preferred_element_type=jnp.float32)
        .reshape(rows, cols, heads_here)
        .transpose(2, 0, 1)
    )
    keys_all, values_all = sent_together((keys, values), "col", 1, 0)
    column_bias = collect(bias_local, "row", 1)
    bias_here = lax.all_to_all(column_bias, "col", split_axis=1, concat_axis=2, tiled=True)
    chain_here = lax.dynamic_slice_in_dim(chain, col_index * cols, cols, 0)
    same = (chain_here[:, None] == chain[None, :]).astype(jnp.float32)
    bias_here = (
        bias_here
        + chain_bias[:, None, None] * same[None]
        + (valid[None, None, :] - 1.0) * 1000000000.0
    )

    def attend(block):
        block_query, block_keys, block_values = block
        scores = (
            jnp.einsum(
                "ajhd,akhd->ahjk", block_query, block_keys, preferred_element_type=jnp.float32
            )
            + bias_here[None]
        )
        weights = jax.nn.softmax(scores, axis=-1).astype(jnp.bfloat16)
        return jnp.einsum(
            "ahjk,akhd->ajhd", weights, block_values, preferred_element_type=jnp.float32
        )

    attended = lax.map(
        attend,
        (
            query.reshape(rows // 2, 2, cols, heads_here, head_dim),
            keys_all.reshape(rows // 2, 2, total, heads_here, head_dim),
            values_all.reshape(rows // 2, 2, total, heads_here, head_dim),
        ),
    )
    attended = (attended.reshape(rows, cols, spread) * gating).astype(jnp.bfloat16)
    update = jnp.dot(
        attended.reshape(rows * cols, spread), att_out, preferred_element_type=jnp.float32
    ).reshape(rows, cols, width)
    update_half = sum_at_owner(update.astype(jnp.bfloat16), "sub", 1)
    pair_half = lax.dynamic_slice_in_dim(pair, sub_index * half, half, 1).astype(jnp.float32)
    first = pair_half + update_half
    mixed = norm(first).astype(jnp.bfloat16)
    mixed_flat = mixed.reshape(rows * half, width)
    quad = jnp.dot(mixed_flat, mult_in, preferred_element_type=jnp.float32).reshape(
        rows, half, 4, mult_width
    )
    row_valid = lax.dynamic_slice_in_dim(valid, row_index * rows, rows, 0)
    col_valid = lax.dynamic_slice_in_dim(valid, col_index * cols + sub_index * half, half, 0)
    outer = row_valid[:, None, None] * col_valid[None, :, None]
    left = (outer * jax.nn.sigmoid(quad[:, :, 1]) * quad[:, :, 0]).astype(jnp.bfloat16)
    right = (outer * jax.nn.sigmoid(quad[:, :, 3]) * quad[:, :, 2]).astype(jnp.bfloat16)
    gate_out = jax.nn.sigmoid(jnp.dot(mixed_flat, mult_gate, preferred_element_type=jnp.float32))
    partial_value = jnp.einsum(
        "ikc,jkc->ijc",
        left,
        lax.all_gather(right, "row", axis=0, tiled=True),
        preferred_element_type=jnp.float32,
    )
    tri = sum_at_owner(partial_value.astype(jnp.bfloat16), ("col", "sub"), 1)
    tri_normed = norm(tri).astype(jnp.bfloat16).reshape(rows * half, mult_width)
    second = first + (
        gate_out * jnp.dot(tri_normed, mult_out, preferred_element_type=jnp.float32)
    ).reshape(rows, half, width)
    last_normed = norm(second).astype(jnp.bfloat16).reshape(rows * half, width)
    hidden = jax.nn.relu(jnp.dot(last_normed, trans_up, preferred_element_type=jnp.float32)).astype(
        jnp.bfloat16
    )
    result = second + jnp.dot(hidden, trans_down, preferred_element_type=jnp.float32).reshape(
        rows, half, width
    )
    return result.astype(jnp.bfloat16)


def solution(mesh):
    placed = (
        P(("grp", "row"), "col", None),
        P("grp"),
        P("grp"),
        P(None, None, "sub"),
        P(None, "sub"),
        P("sub"),
        P("sub", None),
        P(),
        P(),
        P(),
        P(),
        P(),
    )
    return jax.shard_map(
        local,
        mesh=mesh,
        in_specs=placed,
        out_specs=P(("grp", "row"), ("col", "sub"), None),
        check_vma=False,
    )
```

profile of v0, /device:TPU:33, one launch (start us, length us, event | category | flops | bytes accessed | tf_op | source)
XLA Modules:
  0.0 350.1 jit_solution(3556476479673316180)
XLA Ops:
  6.6 1.2 convert_reduce_fusion.2
  7.8 1.4 fusion.28
  9.2 1.4 convolution_bitcast_fusion.1
  10.7 0.9 broadcast_in_dim.8
  11.5 46.3 %all-to-all-start = ((f32[32,2,12,96]{3,1,2,0:T(2,128)}), f32[32,2,12,96]{3,1,2,0:T(2,128)}, u32[]{:S(2)}, u32[]{:S(2)}) async-start(f32[32,2,12,96]{3,1,2,0:T(2,128)} %broadcast_in_dim.8), calls=%async_computation | async-start | bytes 786432 | tf_op jit(solution)/shard_map/all_to_all | solution.py:24
  58.0 0.9 fusion.79
  59.0 1.2 copy.71
  61.5 47.7 %all-to-all-done = f32[32,2,12,96]{3,1,2,0:T(2,128)} async-done(((f32[32,2,12,96]{3,1,2,0:T(2,128)}), f32[32,2,12,96]{3,1,2,0:T(2,128)}, u32[]{:S(2)}, u32[]{:S(2)}) %all-to-all-start) | async-done | bytes 294944 | tf_op jit(solution)/shard_map/all_to_all | solution.py:24
  109.2 4.3 %all-to-all-start.1 = ((f32[2,384,96]{2,0,1:T(2,128)}), f32[2,384,96]{2,0,1:T(2,128)S(1)}, u32[]{:S(2)}, u32[]{:S(2)}) async-start(f32[2,384,96]{2,0,1:T(2,128)} %bitcast.19), calls=%async_computation.1 | async-start | bytes 786432 | tf_op jit(solution)/shard_map/all_to_all | solution.py:94
  113.5 3.7 %fusion.78 = (bf16[12,384,64]{2,0,1:T(8,128)(2,1)S(1)}, bf16[12,384,64]{2,0,1:T(8,128)(2,1)}) fusion(bf16[24,384,64]{2,0,1:T(8,128)(2,1)} %all-gather.3.cloned.1.call-done), kind=kLoop, calls=%fused_computation.111 | loop fusion | bytes 2359296 | tf_op jit(solution)/shard_map/split | solution.py:13
  117.3 2.6 copy.91
  119.9 1.5 copy.92
  122.4 14.8 %while.10 = (s32[]{:T(128)}, f32[6,2,96,2,32]{2,4,3,1,0:T(8,128)S(1)}, bf16[6,2,384,2,32]{2,4,3,1,0:T(8,128)(2,1)}, bf16[6,2,96,2,32]{2,4,3,1,0:T(8,128)(2,1)S(1...) while((s32[]{:T(128)}, f32[6,2,96,2,32]{2,4,3,1,0:T(8,128)S(1)}, ...), condition=%wide.region_5.6_spmd, body=%wide.region_2.5_spmd.sunk | while | flops 29344896 | bytes 2792013 | solution.py:116
  122.7 0.5 fusion.105
  123.2 1.7 fusion.106
  125.6 1.7 fusion.106
  128.1 1.7 fusion.106
  130.6 1.7 fusion.106
  133.0 1.7 fusion.106
  135.5 1.7 fusion.106
  137.2 1.3 convolution_convert_fusion.1
  138.6 6.7 %all_to_all.33 = bf16[2,12,48,128]{3,2,1,0:T(8,128)(2,1)S(1)} all-to-all(bf16[2,12,48,128]{3,2,1,0:T(8,128)(2,1)S(1)} %bitcast.193), channel_id=1, replica_groups=mesh['grp'=2,'row'=32,'col'=4,'sub'=2] {'sub'}, dimensions={0} | all-to-all | bytes 589824 | tf_op jit(solution)/shard_map/all_to_all | solution.py:40
  146.0 0.7 copy-done.3
  147.0 0.8 fusion.39
  148.3 121.5 %all-gather.5.cloned.1.call-done = bf16[384,48,128]{2,1,0:T(8,128)(2,1)} async-done(((bf16[12,48,128]{2,1,0:T(8,128)(2,1)}), bf16[384,48,128]{2,1,0:T(8,128)(2,1)}) %all-gather.5.cloned.1.call-update) | async-done | bytes 4718608 | tf_op jit(solution)/shard_map/all_gather | solution.py:145
  269.9 17.9 %copy.81 = bf16[384,48,128]{1,0,2:T(8,128)(2,1)} copy(bf16[384,48,128]{2,1,0:T(8,128)(2,1)} %all-gather.5.cloned.1.call-done) | data formatting | bytes 9437184 | tf_op jit(solution)/shard_map/all_gather | solution.py:145
  287.8 9.0 %fusion.20 = bf16[12,384,128]{1,0,2:T(8,128)(2,1)S(1)} fusion(bf16[384,48,128]{1,0,2:T(8,128)(2,1)} %copy.81, bf16[12,48,128]{1,0,2:T(8,128)(2,1)S(1)} %copy.82), kind=kOutput, calls=%fused_computation.21 | convolution fusion | flops 57212928 | bytes 6045696 | tf_op jit(solution)/shard_map/ikc,jkc->ijc/dot_general | solution.py:142
  296.8 1.3 copy.83
  298.1 1.1 copy.84
  299.2 24.6 %all-to-all-start.3 = ((bf16[8,12,48,128]{3,2,1,0:T(8,128)(2,1)}), bf16[8,12,48,128]{3,2,1,0:T(8,128)(2,1)S(1)}, u32[]{:S(2)}, u32[]{:S(2)}) async-start(bf16[8,12,48,128]{3,2,1,0:T(8,128)(2,1)} %copy.84), calls=%async_computation.3 | async-start | bytes 2359296 | tf_op jit(solution)/shard_map/all_to_all | solution.py:40
  324.1 16.1 %all-to-all-done.3 = bf16[8,12,48,128]{3,2,1,0:T(8,128)(2,1)S(1)} async-done(((bf16[8,12,48,128]{3,2,1,0:T(8,128)(2,1)}), bf16[8,12,48,128]{3,2,1,0:T(8,128)(2,1)S(1)}, u32[]{:S(2)}, u32[]{:S(2)}) %all-to-all-start.3) | async-done | bytes 1179680 | tf_op jit(solution)/shard_map/all_to_all | solution.py:40
  342.5 0.7 add_convert_fusion
  (85 shorter events, 9.9 us)
Async XLA Ops:
  6.5 335.5 %copy-start = (bf16[512,128]{1,0:T(8,128)(2,1)S(1)}, bf16[512,128]{1,0:T(8,128)(2,1)}, u32[]{:S(2)}) copy-start(bf16[512,128]{1,0:T(8,128)(2,1)} %param.25) | copy-start | bytes 393220
  6.6 51.4 %copy-start.1 = (bf16[12,96,128]{2,1,0:T(8,128)(2,1)S(1)}, bf16[12,96,128]{2,1,0:T(8,128)(2,1)}, u32[]{:S(2)}) copy-start(bf16[12,96,128]{2,1,0:T(8,128)(2,1)} %param.14) | copy-start | bytes 884740
  6.6 51.4 %copy-start.6 = (bf16[128,4,64]{0,2,1:T(8,128)(2,1)S(1)}, bf16[128,4,64]{0,2,1:T(8,128)(2,1)}, u32[]{:S(2)}) copy-start(bf16[128,4,64]{0,2,1:T(8,128)(2,1)} %param.17) | copy-start | bytes 196612
  11.5 97.7 %all-to-all-start = ((f32[32,2,12,96]{3,1,2,0:T(2,128)}), f32[32,2,12,96]{3,1,2,0:T(2,128)}, u32[]{:S(2)}, u32[]{:S(2)}) async-start(f32[32,2,12,96]{3,1,2,0:T(2,128)} %broadcast_in_dim.8), calls=%async_computation | async-start | bytes 786432 | tf_op jit(solution)/shard_map/all_to_all | solution.py:24
  57.9 55.7 %all-gather.3.cloned.1.call-start = ((), (), s32[]{:S(2)}) async-start(), calls=%async_computation.4 | async-start | bytes 2949120 | tf_op jit(solution)/shard_map/all_gather | solution.py:13
  58.8 2.6 copy-start.2
  58.9 2.1 copy-start.5
  58.9 2.3 copy-start.8
  109.2 12.2 %all-to-all-start.1 = ((f32[2,384,96]{2,0,1:T(2,128)}), f32[2,384,96]{2,0,1:T(2,128)S(1)}, u32[]{:S(2)}, u32[]{:S(2)}) async-start(f32[2,384,96]{2,0,1:T(2,128)} %bitcast.19), calls=%async_computation.1 | async-start | bytes 786432 | tf_op jit(solution)/shard_map/all_to_all | solution.py:94
  113.5 156.3 %all-gather.5.cloned.1.call-start = ((), (), s32[]{:S(2)}) async-start(), calls=%async_computation.5 | async-start | bytes 4866048 | tf_op jit(solution)/shard_map/all_gather | solution.py:145
  119.9 2.0 copy-start.9
  121.4 1.0 copy-start.13
  122.4 14.8 %copy-start.12 = (bf16[64,128]{1,0:T(8,128)(2,1)S(1)}, bf16[64,128]{1,0:T(8,128)(2,1)}, u32[]{:S(2)}) copy-start(bf16[64,128]{1,0:T(8,128)(2,1)} %param.20) | copy-start | bytes 49156
  146.0 0.7 copy-start.3
  299.2 24.6 %copy-start.4 = (bf16[12,48,128]{2,1,0:T(8,128)(2,1)S(1)}, bf16[12,48,128]{2,1,0:T(8,128)(2,1)}, u32[]{:S(2)}) copy-start(bf16[12,48,128]{2,1,0:T(8,128)(2,1)} %copy-done.3) | copy-start | bytes 442372
  299.2 24.6 %copy-start.11 = (bf16[128,128]{1,0:T(8,128)(2,1)S(1)}, bf16[128,128]{1,0:T(8,128)(2,1)}, u32[]{:S(2)}) copy-start(bf16[128,128]{1,0:T(8,128)(2,1)} %param.22) | copy-start | bytes 98308
  299.2 41.0 %all-to-all-start.3 = ((bf16[8,12,48,128]{3,2,1,0:T(8,128)(2,1)}), bf16[8,12,48,128]{3,2,1,0:T(8,128)(2,1)S(1)}, u32[]{:S(2)}, u32[]{:S(2)}) async-start(bf16[8,12,48,128]{3,2,1,0:T(8,128)(2,1)} %copy.84), calls=%async_computation.3 | async-start | bytes 2359296 | tf_op jit(solution)/shard_map/all_to_all | solution.py:40
  323.9 17.3 %copy-start.7 = (bf16[128,128]{1,0:T(8,128)(2,1)S(1)}, bf16[128,128]{1,0:T(8,128)(2,1)}, u32[]{:S(2)}) copy-start(bf16[128,128]{1,0:T(8,128)(2,1)} %param.23) | copy-start | bytes 98308
  340.8 1.2 copy-start.10
Sparse Core Ops, SparseCore 0:
  60.8 50.1 all-gather.2
  148.0 121.8 all-gather.4
where the time goes:
time: 351 us; the launch traced here: 350 us
  waiting for transfers between devices  185 us (53%)
  starting transfers between devices  75.3 us (21%)
  local copies, waits for them, and re-layouts  32.7 us (9%)
  matrix products  28.6 us (8%)
  between operations  14.5 us (4%)
  other arithmetic  6.71 us (2%)
  blocking collectives  6.71 us (2%)
    all_gather x1, waiting for transfers between devices, local(): lax.all_gather(right, 'row', axis=0, tiled=True)  122 us
    all_to_all x1, waiting for transfers between devices, copy_for_each(): lax.all_to_all(jnp.broadcast_to(shard[None], (devices, *shard.shape)), ax...  47.7 us
    all_to_all x1, starting transfers between devices, copy_for_each(): lax.all_to_all(jnp.broadcast_to(shard[None], (devices, *shard.shape)), ax...  46.3 us
    all_to_all x1, starting transfers between devices, sum_at_owner(): lax.all_to_all(cut_along(shard, dim, devices), axis, 0, 0, tiled=True)  24.6 us
    all_gather x1, local copies, waits for them, and re-layouts, local(): lax.all_gather(right, 'row', axis=0, tiled=True)  17.9 us
    all_to_all x1, waiting for transfers between devices, sum_at_owner(): lax.all_to_all(cut_along(shard, dim, devices), axis, 0, 0, tiled=True)  16.1 us
    dot_general x6, matrix products, attend(): jnp.einsum('ahjk,akhd->ajhd', weights, block_values, preferred_element_ty...  10.1 us
    dot_general x1, matrix products, local(): jnp.einsum('ikc,jkc->ijc', left, lax.all_gather(right, 'row', axis=0, til...  9.04 us
  transfers between devices with their start and end apart: 5, of which 3 were waited for; matrix products, arithmetic and copies ran while one was open for 3% of the time, Pallas kernels for 0%

commit v1 on v0

--- a/solution.py
+++ b/solution.py
@@ -142,7 +142,9 @@
     partial_value = jnp.einsum(
         "ikc,jkc->ijc",
         left,
-        lax.all_gather(right, "row", axis=0, tiled=True),
+        jnp.concatenate(
+            lax.all_to_all(jnp.stack([right] * lax.axis_size("row")), "row", 0, 0), axis=0
+        ),
         preferred_element_type=jnp.float32,
     )
     tri = sum_at_owner(partial_value.astype(jnp.bfloat16), ("col", "sub"), 1)

time: 351 us -> 635 us (1.81); the launches traced: 350 us -> 623 us
  waiting for transfers between devices: 185 us -> 470 us
  local copies, waits for them, and re-layouts: 32.7 us -> 25.6 us
    all_to_all x0 -> x1, waiting for transfers between devices: none -> 406 us  [local(): lax.all_to_all(jnp.stack([right] * lax.axis_size('row')), 'row', 0, 0)]
    all_gather x1 -> x0, waiting for transfers between devices: 122 us -> none  [local(): lax.all_gather(right, 'row', axis=0, tiled=True)]
    all_to_all x0 -> x1, starting transfers between devices: none -> 22.9 us  [local(): lax.all_to_all(jnp.stack([right] * lax.axis_size('row')), 'row', 0, 0)]
    all_to_all x1, starting transfers between devices: 24.6 us -> 4.51 us  [sum_at_owner(): lax.all_to_all(cut_along(shard, dim, devices), axis, 0, 0, tiled=True)]
    all_gather x1 -> x0, local copies, waits for them, and re-layouts: 17.9 us -> none  [local(): lax.all_gather(right, 'row', axis=0, tiled=True)]
    reshape x0 -> x1, local copies, waits for them, and re-layouts: none -> 7.59 us  [local(): jnp.concatenate(lax.all_to_all(jnp.stack([right] * lax.axis_size('row')),...]
  transfers between devices with their start and end apart: 5 -> 5, of which waited for: 3 -> 3; matrix products, arithmetic and copies ran while one was open for 3% -> 2% of each run, Pallas kernels for 0% -> 0%
where the time goes in v1:
time: 635 us; the launch traced here: 623 us
  waiting for transfers between devices  470 us (74%)
  starting transfers between devices  78.1 us (12%)
  local copies, waits for them, and re-layouts  25.6 us (4%)
  matrix products  22.8 us (4%)
  between operations  14.5 us (2%)
  blocking collectives  6.65 us (1%)
    all_to_all x1, waiting for transfers between devices, local(): lax.all_to_all(jnp.stack([right] * lax.axis_size('row')), 'row', 0, 0)  406 us
    all_to_all x1, waiting for transfers between devices, copy_for_each(): lax.all_to_all(jnp.broadcast_to(shard[None], (devices, *shard.shape)), ax...  47.7 us
    all_to_all x1, starting transfers between devices, copy_for_each(): lax.all_to_all(jnp.broadcast_to(shard[None], (devices, *shard.shape)), ax...  46.3 us
    all_to_all x1, starting transfers between devices, local(): lax.all_to_all(jnp.stack([right] * lax.axis_size('row')), 'row', 0, 0)  22.9 us
    all_to_all x1, waiting for transfers between devices, sum_at_owner(): lax.all_to_all(cut_along(shard, dim, devices), axis, 0, 0, tiled=True)  16.2 us
  transfers between devices with their start and end apart: 5, of which 3 were waited for; matrix products, arithmetic and copies ran while one was open for 2% of the time, Pallas kernels for 0%

profile of v1, /device:TPU:33, one launch (start us, length us, event | category | flops | bytes accessed | tf_op | source)
XLA Modules:
  0.0 623.4 jit_solution(7619828534249152553)
XLA Ops:
  6.6 1.2 convert_reduce_fusion.2
  7.8 1.4 fusion.28
  9.2 1.4 convolution_bitcast_fusion.1
  10.7 0.9 broadcast_in_dim.8
  11.5 46.3 %all-to-all-start = ((f32[32,2,12,96]{3,1,2,0:T(2,128)}), f32[32,2,12,96]{3,1,2,0:T(2,128)}, u32[]{:S(2)}, u32[]{:S(2)}) async-start(f32[32,2,12,96]{3,1,2,0:T(2,128)} %broadcast_in_dim.8), calls=%async_computation | async-start | bytes 786432 | tf_op jit(solution)/shard_map/all_to_all | solution.py:24
  58.0 0.9 fusion.79
  59.0 1.2 copy.71
  61.5 47.7 %all-to-all-done = f32[32,2,12,96]{3,1,2,0:T(2,128)} async-done(((f32[32,2,12,96]{3,1,2,0:T(2,128)}), f32[32,2,12,96]{3,1,2,0:T(2,128)}, u32[]{:S(2)}, u32[]{:S(2)}) %all-to-all-start) | async-done | bytes 294944 | tf_op jit(solution)/shard_map/all_to_all | solution.py:24
  109.2 4.3 all-to-all-start.1
  113.5 3.7 fusion.78
  117.3 2.6 copy.91
  119.9 1.5 copy.92
  122.4 14.8 %while.10 = (s32[]{:T(128)}, f32[6,2,96,2,32]{2,4,3,1,0:T(8,128)S(1)}, bf16[6,2,384,2,32]{2,4,3,1,0:T(8,128)(2,1)}, bf16[6,2,96,2,32]{2,4,3,1,0:T(8,128)(2,1)S(1...) while((s32[]{:T(128)}, f32[6,2,96,2,32]{2,4,3,1,0:T(8,128)S(1)}, ...), condition=%wide.region_5.6_spmd, body=%wide.region_2.5_spmd.sunk | while | flops 29344896 | bytes 2792013 | solution.py:116
  123.2 1.7 fusion.106
  125.6 1.7 fusion.106
  128.1 1.7 fusion.106
  130.6 1.7 fusion.106
  133.0 1.7 fusion.106
  135.5 1.7 fusion.106
  137.2 1.3 convolution_convert_fusion.1
  138.5 6.6 %all_to_all.38 = bf16[2,12,48,128]{3,2,1,0:T(8,128)(2,1)S(1)} all-to-all(bf16[2,12,48,128]{3,2,1,0:T(8,128)(2,1)S(1)} %bitcast.194), channel_id=1, replica_groups=mesh['grp'=2,'row'=32,'col'=4,'sub'=2] {'sub'}, dimensions={0} | all-to-all | bytes 589824 | tf_op jit(solution)/shard_map/all_to_all | solution.py:40
  146.0 0.7 copy-done.3
  147.1 3.2 stack.2
  150.4 22.9 %all-to-all-start.3 = ((bf16[32,12,48,128]{3,2,1,0:T(8,128)(2,1)}), bf16[32,12,48,128]{3,2,1,0:T(8,128)(2,1)}, u32[]{:S(2)}, u32[]{:S(2)}) async-start(bf16[32,12,48,128]{3,2,1,0:T(8,128)(2,1)} %stack.2), calls=%async_computation.3 | async-start | bytes 9437184 | tf_op jit(solution)/shard_map/all_to_all | solution.py:146
  173.7 405.6 %all-to-all-done.3 = bf16[32,12,48,128]{3,2,1,0:T(8,128)(2,1)} async-done(((bf16[32,12,48,128]{3,2,1,0:T(8,128)(2,1)}), bf16[32,12,48,128]{3,2,1,0:T(8,128)(2,1)}, u32[]{:S(2)}, u32[]{:S(2)}) %all-to-all-start.3) | async-done | bytes 4718624 | tf_op jit(solution)/shard_map/all_to_all | solution.py:146
  579.3 7.6 %copy.81 = bf16[384,48,128]{0,1,2:T(8,128)(2,1)} copy(bf16[384,48,128]{2,1,0:T(8,128)(2,1)} %bitcast.37) | data formatting | bytes 9437184 | tf_op jit(solution)/shard_map/reshape | solution.py:145
  586.9 3.3 fusion.20
  590.2 1.3 copy.83
  591.5 1.1 copy.84
  592.6 4.5 all-to-all-start.4
  597.3 16.2 %all-to-all-done.4 = bf16[8,12,48,128]{3,2,1,0:T(8,128)(2,1)S(1)} async-done(((bf16[8,12,48,128]{3,2,1,0:T(8,128)(2,1)}), bf16[8,12,48,128]{3,2,1,0:T(8,128)(2,1)S(1)}, u32[]{:S(2)}, u32[]{:S(2)}) %all-to-all-start.4) | async-done | bytes 1179680 | tf_op jit(solution)/shard_map/all_to_all | solution.py:40
  615.8 0.7 add_convert_fusion
  (85 shorter events, 10.5 us)
Async XLA Ops:
  6.5 608.8 %copy-start = (bf16[512,128]{1,0:T(8,128)(2,1)S(1)}, bf16[512,128]{1,0:T(8,128)(2,1)}, u32[]{:S(2)}) copy-start(bf16[512,128]{1,0:T(8,128)(2,1)} %param.25) | copy-start | bytes 393220
  6.6 51.4 %copy-start.1 = (bf16[12,96,128]{2,1,0:T(8,128)(2,1)S(1)}, bf16[12,96,128]{2,1,0:T(8,128)(2,1)}, u32[]{:S(2)}) copy-start(bf16[12,96,128]{2,1,0:T(8,128)(2,1)} %param.14) | copy-start | bytes 884740
  6.6 51.4 %copy-start.6 = (bf16[128,4,64]{0,2,1:T(8,128)(2,1)S(1)}, bf16[128,4,64]{0,2,1:T(8,128)(2,1)}, u32[]{:S(2)}) copy-start(bf16[128,4,64]{0,2,1:T(8,128)(2,1)} %param.17) | copy-start | bytes 196612
  11.5 97.7 %all-to-all-start = ((f32[32,2,12,96]{3,1,2,0:T(2,128)}), f32[32,2,12,96]{3,1,2,0:T(2,128)}, u32[]{:S(2)}, u32[]{:S(2)}) async-start(f32[32,2,12,96]{3,1,2,0:T(2,128)} %broadcast_in_dim.8), calls=%async_computation | async-start | bytes 786432 | tf_op jit(solution)/shard_map/all_to_all | solution.py:24
  57.9 55.7 %all-gather.2.cloned.1.call-start = ((), (), s32[]{:S(2)}) async-start(), calls=%async_computation.5 | async-start | bytes 2949120 | tf_op jit(solution)/shard_map/all_gather | solution.py:13
  58.8 2.6 copy-start.2
  58.9 2.1 copy-start.5
  58.9 2.3 copy-start.8
  109.2 12.2 %all-to-all-start.1 = ((f32[2,384,96]{2,0,1:T(2,128)}), f32[2,384,96]{2,0,1:T(2,128)S(1)}, u32[]{:S(2)}, u32[]{:S(2)}) async-start(f32[2,384,96]{2,0,1:T(2,128)} %bitcast.19), calls=%async_computation.1 | async-start | bytes 786432 | tf_op jit(solution)/shard_map/all_to_all | solution.py:94
  119.9 2.0 copy-start.9
  121.4 1.0 copy-start.13
  122.4 14.8 %copy-start.12 = (bf16[64,128]{1,0:T(8,128)(2,1)S(1)}, bf16[64,128]{1,0:T(8,128)(2,1)}, u32[]{:S(2)}) copy-start(bf16[64,128]{1,0:T(8,128)(2,1)} %param.20) | copy-start | bytes 49156
  145.9 0.7 copy-start.3
  150.4 429.0 %all-to-all-start.3 = ((bf16[32,12,48,128]{3,2,1,0:T(8,128)(2,1)}), bf16[32,12,48,128]{3,2,1,0:T(8,128)(2,1)}, u32[]{:S(2)}, u32[]{:S(2)}) async-start(bf16[32,12,48,128]{3,2,1,0:T(8,128)(2,1)} %stack.2), calls=%async_computation.3 | async-start | bytes 9437184 | tf_op jit(solution)/shard_map/all_to_all | solution.py:146
  592.6 4.5 copy-start.4
  592.6 4.5 copy-start.11
  592.6 21.0 %all-to-all-start.4 = ((bf16[8,12,48,128]{3,2,1,0:T(8,128)(2,1)}), bf16[8,12,48,128]{3,2,1,0:T(8,128)(2,1)S(1)}, u32[]{:S(2)}, u32[]{:S(2)}) async-start(bf16[8,12,48,128]{3,2,1,0:T(8,128)(2,1)} %copy.84), calls=%async_computation.4 | async-start | bytes 2359296 | tf_op jit(solution)/shard_map/all_to_all | solution.py:40
  597.1 17.4 %copy-start.7 = (bf16[128,128]{1,0:T(8,128)(2,1)S(1)}, bf16[128,128]{1,0:T(8,128)(2,1)}, u32[]{:S(2)}) copy-start(bf16[128,128]{1,0:T(8,128)(2,1)} %param.23) | copy-start | bytes 98308
  614.1 1.2 copy-start.10
Sparse Core Ops, SparseCore 0:
  60.8 50.1 all-gather.1
